TPU v7x, 32 devices: a whole 2x2x4 slice. The times are simulated.
32 devices in a mesh: gene: 4 (over z), var: 4 (over y, core), perm: 2 (over x).
Axes of the slice: x: 2, y: 2, z: 4, core: 2. Of those that a mesh axis runs over, the one named last changes fastest.
Arguments:
- genotypes: bfloat16 [4, 6144, 768], P('gene', ('var', 'perm')), may hold values from 0 to 2
- phenotypes: float32 [512, 768], P('gene'), may hold values from -6 to 6
- perm_rows: int32 [256, 768], P(('var', 'perm')), may hold values from 0 to 767, each once within a row
- starts: int32 [512], P('gene'), may hold values from 0 to 2048, as said below
Outputs:
- maxima: float32 [256, 512], P(('var', 'perm'), 'gene')
- moments: float32 [2, 512], P(None, 'gene')
- pooled: float32 [2], replicated
Inputs may be any that keep to these rules, and one draw needn't show every extreme that they name: `perm_rows`: each row is a permutation of 0 to 767. Within each block of 128 genes the starts never fall; a gene's window of 4096 variants lies inside its block's 6144 variants.
All inputs are finite; a program needn't handle non-finite values.
Results may differ from a plain program's by a relative error of at most 0.0023.
Values may be sent and summed in bfloat16 or wider, within the bound.
A program may use at most 64 MiB of HBM per device.

v0:
```python
import math

import jax
import jax.numpy as jnp
from jax import lax
from jax.sharding import PartitionSpec as P

WINDOW = 4096
PERMS = 256


def standard_rows(values):
    as_float = values.astype(jnp.float32)
    centred = as_float - jnp.mean(as_float, axis=1, keepdims=True)
    inv_norm = lax.rsqrt(jnp.sum(centred * centred, axis=1, keepdims=True) + 1.0)
    return (centred * inv_norm).astype(jnp.bfloat16)


def window_best(row_block, first_row, perm_table, starts):
    scores = lax.dot_general(
        row_block, perm_table, (((1,), (1,)), ((), ())), preferred_element_type=jnp.float32
    )
    row_index = first_row + lax.broadcasted_iota(jnp.int32, (row_block.shape[0], 1, 1), 0)
    inside = (row_index >= starts[None, None, :]) & (row_index < starts[None, None, :] + WINDOW)
    return jnp.max(jnp.where(inside, scores * scores, 0.0), axis=0)


def shards(genotypes, phenotypes, perm_rows, starts):
    standard = standard_rows(genotypes[0])
    table_base = standard_rows(phenotypes).T
    samples = phenotypes.shape[1]
    local_rows = standard.shape[0]
    width_own = perm_rows.shape[0]
    gene_count = phenotypes.shape[0]
    selector = jax.nn.one_hot(perm_rows, samples, dtype=jnp.bfloat16)
    perm_table = jnp.einsum(
        "pst,tg->psg", selector, table_base, preferred_element_type=jnp.float32
    ).astype(jnp.bfloat16)
    start_best = jnp.zeros((width_own, gene_count), jnp.float32)
    shard_rows = lax.all_gather(standard, ("var", "perm"), axis=0, tiled=True)
    step_rows = math.gcd(shard_rows.shape[0], local_rows)

    def one_block(block_step, carried):
        row_block = lax.dynamic_slice_in_dim(shard_rows, block_step * step_rows, step_rows, 0)
        found = window_best(row_block, block_step * step_rows, perm_table, starts)
        return jnp.maximum(carried, found)

    best_sq = lax.fori_loop(0, shard_rows.shape[0] // step_rows, one_block, start_best)
    maxima = best_sq * samples
    log_stat = jnp.log1p(maxima)
    totals = lax.psum(
        (jnp.sum(log_stat, axis=0), jnp.sum(log_stat * log_stat, axis=0)), ("var", "perm")
    )
    moments = jnp.stack(totals) / PERMS
    pooled = lax.psum(jnp.sum(moments, axis=1), "gene") / (gene_count * lax.axis_size("gene"))
    return (maxima, moments, pooled)


def solution(mesh):
    return jax.shard_map(
        shards,
        mesh=mesh,
        in_specs=(
            P("gene", ("var", "perm"), None),
            P("gene", None),
            P(("var", "perm"), None),
            P("gene"),
        ),
        out_specs=(P(("var", "perm"), "gene"), P(None, "gene"), P()),
        check_vma=False,
    )
```

profile of v0, /device:TPU:0, one launch (start us, length us, event | category | flops | bytes accessed | tf_op | source)
XLA Modules:
  0.0 169.1 jit_solution(12829886420838485471)
XLA Ops:
  7.2 0.0 copy-start
  7.2 0.0 copy-start.1
  7.2 0.0 copy-start.3
  7.2 0.0 all-gather.2.cloned.1.call-start
  7.2 1.6 convert_reduce_fusion
  8.9 1.8 %fusion.9 = f32[768]{0:T(1024)S(1)} fusion(bf16[1,768,768]{2,1,0:T(8,128)(2,1)} %param.6, f32[768]{0:T(1024)S(1)} %broadcast_multiply_fusion.1), kind=kLoop, calls=%fused_computation.17 | loop fusion | flops 2358528 | bytes 1185792 | tf_op jit(solution)/shard_map/reduce_sum | solution.py:15
  10.6 0.0 copy-done
  10.7 1.4 fusion.10
  12.0 0.0 all-gather.2.cloned.1.call-update
  12.0 0.0 copy-done.1
  12.1 0.1 reduce_sum.65
  12.2 0.2 multiply_reduce_fusion
  12.4 0.0 copy-done.3
  12.4 0.0 copy-start.2
  12.4 15.2 %fusion.5 = bf16[32,768,128]{2,1,0:T(8,128)(2,1)} fusion(s32[32,768]{1,0:T(8,128)S(1)} %copy-done.3, f32[128,768]{1,0:T(8,128)S(1)} %copy-done.1, f32[128]{0:T(128)S(1)} %add_rsqrt_fusion.1, f32[128]{0:T(128)S(1)} %broadcast_multiply_fusion.3), kind=kOutput, calls=%fused_computation.11 | convolution fusion | flops 4854153216 | bytes 6784000 | tf_op jit(solution)/shard_map/pst,tg->psg/dot_general | solution.py:36
  27.6 46.0 %all-gather.2.cloned.1.call-done = bf16[6144,768]{1,0:T(8,128)(2,1)} async-done(((bf16[768,768]{1,0:T(8,128)(2,1)}), bf16[6144,768]{1,0:T(8,128)(2,1)}) %all-gather.2.cloned.1.call-update) | async-done | bytes 9437200 | tf_op jit(solution)/shard_map/all_gather | solution.py:40
  73.6 0.0 copy-done.2
  73.6 61.8 %while.14 = (s32[]{:T(128)}, f32[32,128]{1,0:T(8,128)S(1)}, s32[128]{0:T(128)S(1)}, bf16[6144,768]{1,0:T(8,128)(2,1)}, bf16[32,768,128]{2,1,0:T(8,128)(2,1)}, /*index=5*/s32[]{:T(128)}, s32[]{:T(128)}, s32[]{:T(128)}, s32[]{:T(128)}) while((s32[]{:T(128)}, f32[32,128]{1,0:T(8,128)S(1)}, s32[128]{0:T(128)S(1)}, ...), condition=%wide.region_6.7_spmd.clone, body=%wide.region_4.6_spmd.clone.sunk | while | flops 4841575424 | bytes 7741605 | solution.py:48
  73.6 0.2 compare_and_fusion.2
  73.8 7.5 %select_reduce_fusion.2 = f32[32,128]{1,0:T(8,128)S(1)} fusion(pred[768,128]{1,0:T(8,128)(4,1)S(1)} %compare_and_fusion.2, bf16[32,768,128]{2,1,0:T(8,128)(2,1)} %get-tuple-element.186, bf16[6144,768]{1,0:T(8,128)(2,1)} %get-tuple-element.185, s32[]{:T(128)S(6)} %select_n.21), kind=kOutput, calls=%fused_computation.clone.1 | convolution fusion | flops 4841271296 | bytes 7585796 | tf_op jit(solution)/shard_map/while/body/eval_jaxpr/dot_general | solution.py:20
  81.4 0.2 compare_and_fusion.2
  81.5 7.5 %select_reduce_fusion.2 = f32[32,128]{1,0:T(8,128)S(1)} fusion(pred[768,128]{1,0:T(8,128)(4,1)S(1)} %compare_and_fusion.2, bf16[32,768,128]{2,1,0:T(8,128)(2,1)} %get-tuple-element.186, bf16[6144,768]{1,0:T(8,128)(2,1)} %get-tuple-element.185, s32[]{:T(128)S(6)} %select_n.21), kind=kOutput, calls=%fused_computation.clone.1 | convolution fusion | flops 4841271296 | bytes 7585796 | tf_op jit(solution)/shard_map/while/body/eval_jaxpr/dot_general | solution.py:20
  89.1 0.2 compare_and_fusion.2
  89.3 7.5 %select_reduce_fusion.2 = f32[32,128]{1,0:T(8,128)S(1)} fusion(pred[768,128]{1,0:T(8,128)(4,1)S(1)} %compare_and_fusion.2, bf16[32,768,128]{2,1,0:T(8,128)(2,1)} %get-tuple-element.186, bf16[6144,768]{1,0:T(8,128)(2,1)} %get-tuple-element.185, s32[]{:T(128)S(6)} %select_n.21), kind=kOutput, calls=%fused_computation.clone.1 | convolution fusion | flops 4841271296 | bytes 7585796 | tf_op jit(solution)/shard_map/while/body/eval_jaxpr/dot_general | solution.py:20
  96.8 0.2 compare_and_fusion.2
  97.0 7.5 %select_reduce_fusion.2 = f32[32,128]{1,0:T(8,128)S(1)} fusion(pred[768,128]{1,0:T(8,128)(4,1)S(1)} %compare_and_fusion.2, bf16[32,768,128]{2,1,0:T(8,128)(2,1)} %get-tuple-element.186, bf16[6144,768]{1,0:T(8,128)(2,1)} %get-tuple-element.185, s32[]{:T(128)S(6)} %select_n.21), kind=kOutput, calls=%fused_computation.clone.1 | convolution fusion | flops 4841271296 | bytes 7585796 | tf_op jit(solution)/shard_map/while/body/eval_jaxpr/dot_general | solution.py:20
  104.6 0.2 compare_and_fusion.2
  104.7 7.5 %select_reduce_fusion.2 = f32[32,128]{1,0:T(8,128)S(1)} fusion(pred[768,128]{1,0:T(8,128)(4,1)S(1)} %compare_and_fusion.2, bf16[32,768,128]{2,1,0:T(8,128)(2,1)} %get-tuple-element.186, bf16[6144,768]{1,0:T(8,128)(2,1)} %get-tuple-element.185, s32[]{:T(128)S(6)} %select_n.21), kind=kOutput, calls=%fused_computation.clone.1 | convolution fusion | flops 4841271296 | bytes 7585796 | tf_op jit(solution)/shard_map/while/body/eval_jaxpr/dot_general | solution.py:20
  112.3 0.2 compare_and_fusion.2
  112.5 7.5 %select_reduce_fusion.2 = f32[32,128]{1,0:T(8,128)S(1)} fusion(pred[768,128]{1,0:T(8,128)(4,1)S(1)} %compare_and_fusion.2, bf16[32,768,128]{2,1,0:T(8,128)(2,1)} %get-tuple-element.186, bf16[6144,768]{1,0:T(8,128)(2,1)} %get-tuple-element.185, s32[]{:T(128)S(6)} %select_n.21), kind=kOutput, calls=%fused_computation.clone.1 | convolution fusion | flops 4841271296 | bytes 7585796 | tf_op jit(solution)/shard_map/while/body/eval_jaxpr/dot_general | solution.py:20
  120.0 0.2 compare_and_fusion.2
  120.2 7.5 %select_reduce_fusion.2 = f32[32,128]{1,0:T(8,128)S(1)} fusion(pred[768,128]{1,0:T(8,128)(4,1)S(1)} %compare_and_fusion.2, bf16[32,768,128]{2,1,0:T(8,128)(2,1)} %get-tuple-element.186, bf16[6144,768]{1,0:T(8,128)(2,1)} %get-tuple-element.185, s32[]{:T(128)S(6)} %select_n.21), kind=kOutput, calls=%fused_computation.clone.1 | convolution fusion | flops 4841271296 | bytes 7585796 | tf_op jit(solution)/shard_map/while/body/eval_jaxpr/dot_general | solution.py:20
  127.8 0.2 compare_and_fusion.2
  127.9 7.5 %select_reduce_fusion.2 = f32[32,128]{1,0:T(8,128)S(1)} fusion(pred[768,128]{1,0:T(8,128)(4,1)S(1)} %compare_and_fusion.2, bf16[32,768,128]{2,1,0:T(8,128)(2,1)} %get-tuple-element.186, bf16[6144,768]{1,0:T(8,128)(2,1)} %get-tuple-element.185, s32[]{:T(128)S(6)} %select_n.21), kind=kOutput, calls=%fused_computation.clone.1 | convolution fusion | flops 4841271296 | bytes 7585796 | tf_op jit(solution)/shard_map/while/body/eval_jaxpr/dot_general | solution.py:20
  135.5 0.6 log-plus-one_reduce_fusion
  136.1 13.3 %all-reduce = (f32[1,128]{1,0:T(1,128)S(1)}, f32[1,128]{1,0:T(1,128)S(1)}) all-reduce(f32[1,128]{1,0:T(1,128)S(1)} %bitcast.26, f32[1,128]{1,0:T(1,128)S(1)} %bitcast.25), channel_id=1, replica_groups=mesh['gene'=4,'var'=4,'perm'=2] {'var','perm'}, use_global_device_ids=true, to_apply=%region_10.11 | all-reduce | flops 256 | bytes 2048 | tf_op jit(solution)/shard_map/psum | solution.py:51
  149.4 0.7 fusion.15
  150.1 11.7 %psum.23 = f32[2]{0:T(128)S(1)} all-reduce(f32[2]{0:T(128)S(1)} %get-tuple-element.130), channel_id=1, replica_groups=mesh['gene'=4,'var'=4,'perm'=2] {'gene'}, use_global_device_ids=true, to_apply=%region_12.13 | all-reduce | flops 2 | bytes 16 | tf_op jit(solution)/shard_map/psum | solution.py:55
  161.8 0.5 broadcast_multiply_fusion.2
  (29 shorter events, 0.1 us)
Async XLA Ops:
  7.2 3.5 %copy-start = (bf16[1,768,768]{2,1,0:T(8,128)(2,1)S(1)}, bf16[1,768,768]{2,1,0:T(8,128)(2,1)}, u32[]{:S(2)}) copy-start(bf16[1,768,768]{2,1,0:T(8,128)(2,1)} %param.6) | copy-start | bytes 3538948
  7.2 4.9 %copy-start.1 = (f32[128,768]{1,0:T(8,128)S(1)}, f32[128,768]{1,0:T(8,128)}, u32[]{:S(2)}) copy-start(f32[128,768]{1,0:T(8,128)} %param.7) | copy-start | bytes 1179652
  7.2 5.2 %copy-start.3 = (s32[32,768]{1,0:T(8,128)S(1)}, s32[32,768]{1,0:T(8,128)}, u32[]{:S(2)}) copy-start(s32[32,768]{1,0:T(8,128)} %param.8) | copy-start | bytes 294916
  7.2 66.4 %all-gather.2.cloned.1.call-start = ((), (), s32[]{:S(2)}) async-start(), calls=%async_computation | async-start | bytes 10616832 | tf_op jit(solution)/shard_map/all_gather | solution.py:40
  12.4 61.2 %copy-start.2 = (s32[128]{0:T(128)S(1)}, s32[128]{0:T(128)}, u32[]{:S(2)}) copy-start(s32[128]{0:T(128)} %param.9) | copy-start | bytes 1540
Sparse Core Ops, SparseCore 0:
  12.2 61.4 all-gather.1
where the time goes:
time: 169 us
  matrix products  75.1 us (44%)
  waiting for transfers between devices  46 us (27%)
  blocking collectives  25 us (15%)
  between operations  14.1 us (8%)
  other arithmetic  8.33 us (5%)
    dot_general x8, matrix products, window_best(): lax.dot_general(row_block, perm_table, (((1,), (1,)), ((), ())), preferre...  59.9 us
    all_gather x1, waiting for transfers between devices, shards(): shard_rows = lax.all_gather(standard, ('var', 'perm'), axis=0, tiled=True)  46 us
    dot_general x1, matrix products, shards(): jnp.einsum('pst,tg->psg', selector, table_base, preferred_element_type=jn...  15.2 us
    psum x1, blocking collectives, shards(): lax.psum((jnp.sum(log_stat, axis=0), jnp.sum(log_stat * log_stat, axis=0)...  13.3 us
    psum x1, blocking collectives, shards(): lax.psum(jnp.sum(moments, axis=1), 'gene')  11.7 us
  transfers between devices with their start and end apart: 1, of which 1 were waited for; matrix products, arithmetic and copies ran while one was open for 9% of the time, Pallas kernels for 0%

commit v1 on v0

v1 whole, which is shorter than its diff:
```python
import functools

import jax
import jax.numpy as jnp
from jax import lax
from jax.experimental import pallas as pl
from jax.experimental.pallas import tpu as pltpu
from jax.sharding import PartitionSpec as P

WINDOW = 4096
MESH = pl.DeviceIdType.MESH
UNROLL = 8


def standard_rows(values):
    as_float = values.astype(jnp.float32)
    centred = as_float - jnp.mean(as_float, axis=1, keepdims=True)
    inv_norm = lax.rsqrt(jnp.sum(centred * centred, axis=1, keepdims=True) + 1.0)
    return (centred * inv_norm).astype(jnp.bfloat16)


def kernel(
    sizes, geno, pheno, perms, starts, maxima, moments, pooled,
    rows, table, base, best, mask, stats, sums,
    send, recv, pass_send, pass_recv, stat_send, stat_recv, sum_send, sum_recv,
):
    n_gene, n_var, n_perm = sizes
    n_block = n_var * n_perm
    chips = n_block // 2
    half = rows.shape[1]
    samples = rows.shape[2]
    width, genes = maxima.shape
    tiles, tile_cols, _ = table.shape
    per_tile = tile_cols // genes
    square = n_var == 4 and n_perm == 2

    gene_at = lax.axis_index("gene")
    var_at = lax.axis_index("var")
    perm_at = lax.axis_index("perm")
    core = lax.rem(var_at, 2)
    chip = (var_at // 2) * n_perm + perm_at
    me = var_at * n_perm + perm_at

    def device_of(chip_at, core_at):
        return {"var": (chip_at // n_perm) * 2 + core_at, "perm": lax.rem(chip_at, n_perm)}

    def block_of(chip_at, core_at):
        return ((chip_at // n_perm) * 2 + core_at) * n_perm + lax.rem(chip_at, n_perm)

    def block_peer(step):
        other = lax.rem(me + step, n_block)
        return {"var": other // n_perm, "perm": lax.rem(other, n_perm)}

    def gene_peer(step):
        return {"gene": lax.rem(gene_at + step, n_gene)}

    barrier = pltpu.get_barrier_semaphore()
    for step in range(1, n_block):
        pl.semaphore_signal(barrier, inc=1, device_id=block_peer(step), device_id_type=MESH)
    for step in range(1, n_gene):
        pl.semaphore_signal(barrier, inc=1, device_id=gene_peer(step), device_id_type=MESH)

    for part in range(2):
        rows[me * 2 + part] = standard_rows(geno[pl.ds(part * half, half), :])
    base[...] = standard_rows(pheno[...])
    best[...] = jnp.zeros_like(best)
    pl.semaphore_wait(barrier, n_block - 1 + n_gene - 1)

    def shift(step, back=False):
        if square:
            flip_y, flip_x = step // 2, step % 2
            y, x = chip // 2, lax.rem(chip, 2)
            y = 1 - y if flip_y else y
            x = 1 - x if flip_x else x
            return y * 2 + x
        return lax.rem(chip + (chips - step if back else step), chips)

    waiting = []

    def start(chunk, target, send_sem, recv_sem):
        copy = pltpu.make_async_remote_copy(
            src_ref=rows.at[chunk], dst_ref=rows.at[chunk], send_sem=send_sem,
            recv_sem=recv_sem, device_id=target, device_id_type=MESH,
        )
        copy.start()
        waiting.append(copy)

    def arrive(chunk, recv_sem):
        pltpu.make_async_remote_copy(
            src_ref=rows.at[chunk], dst_ref=rows.at[chunk], send_sem=send.at[0, 0],
            recv_sem=recv_sem, device_id=partner, device_id_type=MESH,
        ).wait_recv()

    partner = device_of(chip, 1 - core)

    def to_chip(step, part):
        start(me * 2 + part, device_of(shift(step), core), send.at[step, part], recv.at[step, part])

    def to_partner(chunk, step, part):
        start(chunk, partner, pass_send.at[step, part], pass_recv.at[step, part])

    if square:
        to_chip(1, 0)
        to_chip(2, 1)
        to_partner(me * 2, 0, 0)
        to_partner(me * 2 + 1, 0, 1)
        to_chip(1, 1)
        to_chip(2, 0)
    else:
        to_partner(me * 2, 0, 0)
        to_partner(me * 2 + 1, 0, 1)
        for step in range(1, chips):
            for part in range(2):
                to_chip(step, part)

    def build(at, carry):
        for pair in range(per_tile):
            order = perms[pl.ds(at * per_tile + pair, 1), :]
            picked = lax.broadcasted_iota(jnp.int32, (samples, samples), 0) == order
            select = jnp.where(picked, 1.0, 0.0).astype(jnp.bfloat16)
            placed = jnp.dot(base[...], select, preferred_element_type=jnp.float32)
            table[at, pl.ds(pair * genes, genes), :] = placed.astype(jnp.bfloat16)
        return carry

    lax.fori_loop(0, tiles, build, 0)

    unroll = min(UNROLL, tiles)

    def score(chunks):
        def one_chunk(at, carry):
            chunk = chunks[0]
            for place in range(1, len(chunks)):
                chunk = jnp.where(at == place, chunks[place], chunk)
            row = chunk * half + lax.broadcasted_iota(jnp.int32, (half, genes), 0)
            first = starts[...]
            mask[...] = jnp.where((row >= first) & (row < first + WINDOW), 1.0, 0.0)

            def some_tiles(group, inner):
                for place in range(unroll):
                    tile = group * unroll + place
                    found = lax.dot_general(
                        rows[chunk], table[tile], (((1,), (1,)), ((), ())),
                        preferred_element_type=jnp.float32,
                    )
                    for pair in range(per_tile):
                        part = found[:, pair * genes:(pair + 1) * genes]
                        part = part * part * mask[...]
                        top = jnp.max(part.reshape(half // 8, 8, genes), axis=0)
                        slot = tile * per_tile + pair
                        best[slot] = jnp.maximum(best[slot], top)
                return inner

            return lax.fori_loop(0, tiles // unroll, some_tiles, carry)

        lax.fori_loop(0, len(chunks), one_chunk, 0)

    def chunk_at(step, core_at, part):
        return block_of(shift(step, back=True) if step else chip, core_at) * 2 + part

    def stage(arrivals, relay):
        if arrivals[0][0]:
            for step, part in arrivals:
                chunk = chunk_at(step, core, part)
                arrive(chunk, recv.at[step, part])
                if relay:
                    other = 3 - step
                    start(chunk, device_of(shift(other), core), send.at[3, part], recv.at[3, part])
                to_partner(chunk, step, part)
        score([chunk_at(step, core, part) for step, part in arrivals])
        for step, part in arrivals:
            arrive(chunk_at(step, 1 - core, part), pass_recv.at[step, part])
        score([chunk_at(step, 1 - core, part) for step, part in arrivals])

    stage([(0, 0), (0, 1)], False)
    if square:
        stage([(1, 0), (2, 1)], True)
        stage([(1, 1), (2, 0)], False)
        stage([(3, 0), (3, 1)], False)
    else:
        for step in range(1, chips):
            stage([(step, 0), (step, 1)], False)

    top = jnp.max(best[...], axis=1) * samples
    maxima[...] = top
    log_stat = jnp.log1p(top)
    total = jnp.sum(log_stat, axis=0, keepdims=True)
    total_sq = jnp.sum(log_stat * log_stat, axis=0, keepdims=True)
    line = lax.broadcasted_iota(jnp.int32, (8, genes), 0)
    stats[me] = jnp.where(line == 0, total, jnp.where(line == 1, total_sq, 0.0))
    exchange = []
    for step in range(1, n_block):
        copy = pltpu.make_async_remote_copy(
            src_ref=stats.at[me], dst_ref=stats.at[me], send_sem=stat_send.at[step],
            recv_sem=stat_recv.at[step], device_id=block_peer(step), device_id_type=MESH,
        )
        copy.start()
        exchange.append(copy)
    for step, copy in enumerate(exchange, 1):
        other = lax.rem(me + n_block - step, n_block)
        pltpu.make_async_remote_copy(
            src_ref=stats.at[other], dst_ref=stats.at[other], send_sem=stat_send.at[step],
            recv_sem=stat_recv.at[step], device_id=partner, device_id_type=MESH,
        ).wait_recv()
    mean = jnp.sum(stats[...], axis=0) / (width * n_block)
    moments[...] = mean[0:2, :]
    sums[gene_at] = mean
    for step in range(1, n_gene):
        copy = pltpu.make_async_remote_copy(
            src_ref=sums.at[gene_at], dst_ref=sums.at[gene_at], send_sem=sum_send.at[step],
            recv_sem=sum_recv.at[step], device_id=gene_peer(step), device_id_type=MESH,
        )
        copy.start()
        exchange.append(copy)
    for step in range(1, n_gene):
        other = lax.rem(gene_at + n_gene - step, n_gene)
        pltpu.make_async_remote_copy(
            src_ref=sums.at[other], dst_ref=sums.at[other], send_sem=sum_send.at[step],
            recv_sem=sum_recv.at[step], device_id=partner, device_id_type=MESH,
        ).wait_recv()
    whole = jnp.sum(sums[...], axis=0)
    pooled[...] = jnp.sum(whole, axis=1, keepdims=True)[0:2, :] / (genes * n_gene)
    for copy in waiting + exchange:
        copy.wait_send()


def solution(mesh):
    n_gene, n_var, n_perm = (mesh.shape[name] for name in ("gene", "var", "perm"))
    n_block = n_var * n_perm

    def shards(genotypes, phenotypes, perm_rows, starts):
        _, local_rows, samples = genotypes.shape
        genes = phenotypes.shape[0]
        width = perm_rows.shape[0]
        half = local_rows // 2
        per_tile = max(256 // genes, 1)
        tiles = width // per_tile
        chips = n_block // 2
        steps = max(chips, 4)
        dma = pltpu.SemaphoreType.DMA
        vmem = pl.BlockSpec(memory_space=pltpu.VMEM)
        flops = 2 * width * genes * samples * (local_rows * n_block + samples)
        maxima, moments, pooled = pl.pallas_call(
            functools.partial(kernel, (n_gene, n_var, n_perm)),
            out_shape=(
                jax.ShapeDtypeStruct((width, genes), jnp.float32),
                jax.ShapeDtypeStruct((2, genes), jnp.float32),
                jax.ShapeDtypeStruct((2, 1), jnp.float32),
            ),
            in_specs=[vmem] * 4,
            out_specs=(vmem,) * 3,
            scratch_shapes=[
                pltpu.VMEM((n_block * 2, half, samples), jnp.bfloat16),
                pltpu.VMEM((tiles, per_tile * genes, samples), jnp.bfloat16),
                pltpu.VMEM((genes, samples), jnp.bfloat16),
                pltpu.VMEM((width, 8, genes), jnp.float32),
                pltpu.VMEM((half, genes), jnp.float32),
                pltpu.VMEM((n_block, 8, genes), jnp.float32),
                pltpu.VMEM((n_gene, 8, genes), jnp.float32),
                dma((steps, 2)), dma((steps, 2)), dma((steps, 2)), dma((steps, 2)),
                dma((n_block,)), dma((n_block,)), dma((n_gene,)), dma((n_gene,)),
            ],
            compiler_params=pltpu.CompilerParams(
                collective_id=0, has_side_effects=True, vmem_limit_bytes=56 * 1024 * 1024
            ),
            cost_estimate=pl.CostEstimate(
                flops=flops, bytes_accessed=local_rows * samples * 2, transcendentals=0
            ),
        )(genotypes[0], phenotypes, perm_rows, starts.reshape(1, genes))
        return maxima, moments, pooled.reshape(2)

    return jax.shard_map(
        shards,
        mesh=mesh,
        in_specs=(
            P("gene", ("var", "perm"), None),
            P("gene", None),
            P(("var", "perm"), None),
            P("gene"),
        ),
        out_specs=(P(("var", "perm"), "gene"), P(None, "gene"), P()),
        check_vma=False,
    )
```

time: 169 us -> 73.1 us (0.43)
  matrix products: 75.1 us -> 0 us
  Pallas kernels: 0 us -> 68.3 us
  waiting for transfers between devices: 46 us -> 0 us
  blocking collectives: 25 us -> 0 us
  between operations: 14.1 us -> 0.64 us
  other arithmetic: 8.33 us -> 1.28 us
  local copies, waits for them, and re-layouts: 0.02 us -> 2.54 us
    dot_general x9 -> x0, matrix products: 75.1 us -> none  [the longest x8 59.9 us: window_best(): lax.dot_general(row_block, perm_table, (((1,), (1,)), ((), ())), preferre...]
    pallas_call x0 -> x1, Pallas kernels: none -> 68.3 us  [shards(): pl.pallas_call(functools.partial(kernel, (n_gene, n_var, n_perm)), out_sh...]
    all_gather x1 -> x0, waiting for transfers between devices: 46 us -> none  [shards(): shard_rows = lax.all_gather(standard, ('var', 'perm'), axis=0, tiled=True)]
    psum x2 -> x0, blocking collectives: 25 us -> none  [the longest x1 13.3 us: shards(): lax.psum((jnp.sum(log_stat, axis=0), jnp.sum(log_stat * log_stat, axis=0)...]
    reduce_sum x6 -> x0, other arithmetic: 4.96 us -> none  [the longest x2 1.96 us: standard_rows(): jnp.sum(centred * centred, axis=1, keepdims=True) + 1.0]
    unnamed x8 -> x2, local copies, waits for them, and re-layouts: 0.02 us -> 2.54 us
  transfers between devices with their start and end apart: 1 -> 0, of which waited for: 1 -> 0; matrix products, arithmetic and copies ran while one was open for 9% -> 0% of each run, Pallas kernels for 0% -> 0%
where the time goes in v1:
time: 73.1 us; the launch traced here: 72.8 us
  Pallas kernels  68.3 us (93%)
  local copies, waits for them, and re-layouts  2.54 us (3%)
  other arithmetic  1.28 us (2%)
    pallas_call x1, Pallas kernels, shards(): pl.pallas_call(functools.partial(kernel, (n_gene, n_var, n_perm)), out_sh...  68.3 us
    unnamed x2, local copies, waits for them, and re-layouts  2.54 us

profile of v1, /device:TPU:0, one launch (start us, length us, event | category | flops | bytes accessed | tf_op | source)
XLA Modules:
  0.0 72.8 jit_solution(4694859208223342280)
XLA Ops:
  0.6 68.3 %shard_map.67 = (f32[32,128]{1,0:T(8,128)}, f32[2,128]{1,0:T(2,128)}, f32[2,1]{1,0:T(2,128)}) custom-call(bf16[768,768]{1,0:T(8,128)(2,1)} %bitcast.2, f32[128,768]{1,0:T(8,128)} %pheno.1, s32[32,768]{1,0:T(8,128)} %perms.1, s32[1,128]{1,0:T(1,128)} %bitcast.3), custom_call_target="tpu_custom_call" | custom-call | flops 43486543872 | bytes 1179648 | tf_op jit(solution)/shard_map/pallas_call | solution.py:242
  69.0 1.3 %reduce = f32[2]{0:T(128)} reduce(f32[2,1]{1,0:T(2,128)} %get-tuple-element.8, f32[]{:T(128)} %constant.1), dimensions={1}, to_apply=%get-tuple-element.8.reduce_sub_computation | reduce | bytes 20 | tf_op jit(solution)/shard_map/pallas_call | solution.py:242
  70.2 1.3 %copy.9 = f32[32,128]{1,0:T(8,128)} copy(f32[32,128]{1,0:T(8,128)} %get-tuple-element.12) | data formatting | bytes 32768
  71.6 1.2 %copy.10 = f32[2,128]{1,0:T(2,128)} copy(f32[2,128]{1,0:T(2,128)} %get-tuple-element.13) | data formatting | bytes 2048

commit v2 on v1

--- a/solution.py
+++ b/solution.py
@@ -20,16 +20,18 @@
 
 
 def kernel(
-    sizes, geno, pheno, perms, starts, maxima, moments, pooled,
+    sizes, geno, pheno, perms, starts, packed,
     rows, table, base, best, mask, stats, sums,
-    send, recv, pass_send, pass_recv, stat_send, stat_recv, sum_send, sum_recv,
+    send, recv, pass_send, pass_recv, far_send, far_recv, far_pass_send, far_pass_recv,
+    stat_send, stat_recv, sum_send, sum_recv,
 ):
     n_gene, n_var, n_perm = sizes
     n_block = n_var * n_perm
     chips = n_block // 2
-    half = rows.shape[1]
+    quarter = rows.shape[1]
+    half = 2 * quarter
     samples = rows.shape[2]
-    width, genes = maxima.shape
+    width, genes = perms.shape[0], packed.shape[1]
     tiles, tile_cols, _ = table.shape
     per_tile = tile_cols // genes
     square = n_var == 4 and n_perm == 2
@@ -61,7 +63,9 @@
         pl.semaphore_signal(barrier, inc=1, device_id=gene_peer(step), device_id_type=MESH)
 
     for part in range(2):
-        rows[me * 2 + part] = standard_rows(geno[pl.ds(part * half, half), :])
+        ready = standard_rows(geno[pl.ds(part * half, half), :])
+        rows[me * 4 + part * 2] = ready[:quarter]
+        rows[me * 4 + part * 2 + 1] = ready[quarter:]
     base[...] = standard_rows(pheno[...])
     best[...] = jnp.zeros_like(best)
     pl.semaphore_wait(barrier, n_block - 1 + n_gene - 1)
@@ -77,38 +81,43 @@
 
     waiting = []
 
-    def start(chunk, target, send_sem, recv_sem):
+    def start(chunk, count, target, send_sem, recv_sem):
+        piece = rows.at[pl.ds(chunk, count)]
         copy = pltpu.make_async_remote_copy(
-            src_ref=rows.at[chunk], dst_ref=rows.at[chunk], send_sem=send_sem,
+            src_ref=piece, dst_ref=piece, send_sem=send_sem,
             recv_sem=recv_sem, device_id=target, device_id_type=MESH,
         )
         copy.start()
         waiting.append(copy)
 
-    def arrive(chunk, recv_sem):
+    def arrive(chunk, count, recv_sem):
+        piece = rows.at[pl.ds(chunk, count)]
         pltpu.make_async_remote_copy(
-            src_ref=rows.at[chunk], dst_ref=rows.at[chunk], send_sem=send.at[0, 0],
+            src_ref=piece, dst_ref=piece, send_sem=send.at[0, 0],
             recv_sem=recv_sem, device_id=partner, device_id_type=MESH,
         ).wait_recv()
 
     partner = device_of(chip, 1 - core)
 
     def to_chip(step, part):
-        start(me * 2 + part, device_of(shift(step), core), send.at[step, part], recv.at[step, part])
+        start(
+            me * 4 + part * 2, 2, device_of(shift(step), core),
+            send.at[step, part], recv.at[step, part],
+        )
 
     def to_partner(chunk, step, part):
-        start(chunk, partner, pass_send.at[step, part], pass_recv.at[step, part])
+        start(chunk, 2, partner, pass_send.at[step, part], pass_recv.at[step, part])
 
     if square:
         to_chip(1, 0)
         to_chip(2, 1)
-        to_partner(me * 2, 0, 0)
-        to_partner(me * 2 + 1, 0, 1)
+        to_partner(me * 4, 0, 0)
+        to_partner(me * 4 + 2, 0, 1)
         to_chip(1, 1)
         to_chip(2, 0)
     else:
-        to_partner(me * 2, 0, 0)
-        to_partner(me * 2 + 1, 0, 1)
+        to_partner(me * 4, 0, 0)
+        to_partner(me * 4 + 2, 0, 1)
         for step in range(1, chips):
             for part in range(2):
                 to_chip(step, part)
@@ -128,18 +137,20 @@
 
     def score(chunks):
         def one_chunk(at, carry):
-            chunk = chunks[0]
+            pieces = chunks[0]
             for place in range(1, len(chunks)):
-                chunk = jnp.where(at == place, chunks[place], chunk)
-            row = chunk * half + lax.broadcasted_iota(jnp.int32, (half, genes), 0)
+                pieces = [jnp.where(at == place, new, old) for new, old in zip(chunks[place], pieces)]
             first = starts[...]
-            mask[...] = jnp.where((row >= first) & (row < first + WINDOW), 1.0, 0.0)
+            for place, piece in enumerate(pieces):
+                row = piece * quarter + lax.broadcasted_iota(jnp.int32, (quarter, genes), 0)
+                inside = (row >= first) & (row < first + WINDOW)
+                mask[pl.ds(place * quarter, quarter), :] = jnp.where(inside, 1.0, 0.0)
 
             def some_tiles(group, inner):
                 for place in range(unroll):
                     tile = group * unroll + place
                     found = lax.dot_general(
-                        rows[chunk], table[tile], (((1,), (1,)), ((), ())),
+                        jnp.concatenate([rows[piece] for piece in pieces], axis=0), table[tile], (((1,), (1,)), ((), ())),
                         preferred_element_type=jnp.float32,
                     )
                     for pair in range(per_tile):
@@ -155,33 +166,56 @@
         lax.fori_loop(0, len(chunks), one_chunk, 0)
 
     def chunk_at(step, core_at, part):
-        return block_of(shift(step, back=True) if step else chip, core_at) * 2 + part
+        return block_of(shift(step, back=True) if step else chip, core_at) * 4 + part * 2
+
+    def halves(arrivals, core_at):
+        found = [chunk_at(step, core_at, part) for step, part in arrivals]
+        return [(chunk, chunk + 1) for chunk in found]
 
     def stage(arrivals, relay):
         if arrivals[0][0]:
             for step, part in arrivals:
                 chunk = chunk_at(step, core, part)
-                arrive(chunk, recv.at[step, part])
+                arrive(chunk, 2, recv.at[step, part])
                 if relay:
-                    other = 3 - step
-                    start(chunk, device_of(shift(other), core), send.at[3, part], recv.at[3, part])
+                    target = device_of(shift(3 - step), core)
+                    for piece in range(2):
+                        start(
+                            chunk + piece, 1, target,
+                            far_send.at[part, piece], far_recv.at[part, piece],
+                        )
                 to_partner(chunk, step, part)
-        score([chunk_at(step, core, part) for step, part in arrivals])
+        score(halves(arrivals, core))
         for step, part in arrivals:
-            arrive(chunk_at(step, 1 - core, part), pass_recv.at[step, part])
-        score([chunk_at(step, 1 - core, part) for step, part in arrivals])
+            arrive(chunk_at(step, 1 - core, part), 2, pass_recv.at[step, part])
+        score(halves(arrivals, 1 - core))
+
+    def far_stage(piece):
+        own = [chunk_at(3, core, part) + piece for part in range(2)]
+        passed = [chunk_at(3, 1 - core, part) + piece for part in range(2)]
+        for part in range(2):
+            arrive(own[part], 1, far_recv.at[part, piece])
+            start(
+                own[part], 1, partner,
+                far_pass_send.at[part, piece], far_pass_recv.at[part, piece],
+            )
+        score([own])
+        for part in range(2):
+            arrive(passed[part], 1, far_pass_recv.at[part, piece])
+        score([passed])
 
     stage([(0, 0), (0, 1)], False)
     if square:
         stage([(1, 0), (2, 1)], True)
         stage([(1, 1), (2, 0)], False)
-        stage([(3, 0), (3, 1)], False)
+        far_stage(0)
+        far_stage(1)
     else:
         for step in range(1, chips):
             stage([(step, 0), (step, 1)], False)
 
     top = jnp.max(best[...], axis=1) * samples
-    maxima[...] = top
+    packed[pl.ds(0, width), :] = top
     log_stat = jnp.log1p(top)
     total = jnp.sum(log_stat, axis=0, keepdims=True)
     total_sq = jnp.sum(log_stat * log_stat, axis=0, keepdims=True)
@@ -202,7 +236,6 @@
             recv_sem=stat_recv.at[step], device_id=partner, device_id_type=MESH,
         ).wait_recv()
     mean = jnp.sum(stats[...], axis=0) / (width * n_block)
-    moments[...] = mean[0:2, :]
     sums[gene_at] = mean
     for step in range(1, n_gene):
         copy = pltpu.make_async_remote_copy(
@@ -218,9 +251,19 @@
             recv_sem=sum_recv.at[step], device_id=partner, device_id_type=MESH,
         ).wait_recv()
     whole = jnp.sum(sums[...], axis=0)
-    pooled[...] = jnp.sum(whole, axis=1, keepdims=True)[0:2, :] / (genes * n_gene)
+    overall = jnp.sum(whole, axis=1, keepdims=True) / (genes * n_gene)
+    spread = pltpu.roll(jnp.broadcast_to(overall, (8, genes)), 2, 0)
+    packed[pl.ds(width, 8), :] = jnp.where(line < 2, mean, spread)
     for copy in waiting + exchange:
         copy.wait_send()
+
+
+def unpack(packed, maxima, moments, pooled):
+    width = maxima.shape[0]
+    maxima[...] = packed[pl.ds(0, width), :]
+    moments[...] = packed[pl.ds(width, 2), :]
+    for place in range(2):
+        pooled[place] = packed[width + 2 + place, 0]
 
 
 def solution(mesh):
@@ -231,7 +274,7 @@
         _, local_rows, samples = genotypes.shape
         genes = phenotypes.shape[0]
         width = perm_rows.shape[0]
-        half = local_rows // 2
+        quarter = local_rows // 4
         per_tile = max(256 // genes, 1)
         tiles = width // per_tile
         chips = n_block // 2
@@ -239,24 +282,21 @@
         dma = pltpu.SemaphoreType.DMA
         vmem = pl.BlockSpec(memory_space=pltpu.VMEM)
         flops = 2 * width * genes * samples * (local_rows * n_block + samples)
-        maxima, moments, pooled = pl.pallas_call(
+        packed = pl.pallas_call(
             functools.partial(kernel, (n_gene, n_var, n_perm)),
-            out_shape=(
-                jax.ShapeDtypeStruct((width, genes), jnp.float32),
-                jax.ShapeDtypeStruct((2, genes), jnp.float32),
-                jax.ShapeDtypeStruct((2, 1), jnp.float32),
-            ),
+            out_shape=jax.ShapeDtypeStruct((width + 8, genes), jnp.float32),
             in_specs=[vmem] * 4,
-            out_specs=(vmem,) * 3,
+            out_specs=vmem,
             scratch_shapes=[
-                pltpu.VMEM((n_block * 2, half, samples), jnp.bfloat16),
+                pltpu.VMEM((n_block * 4, quarter, samples), jnp.bfloat16),
                 pltpu.VMEM((tiles, per_tile * genes, samples), jnp.bfloat16),
                 pltpu.VMEM((genes, samples), jnp.bfloat16),
                 pltpu.VMEM((width, 8, genes), jnp.float32),
-                pltpu.VMEM((half, genes), jnp.float32),
+                pltpu.VMEM((2 * quarter, genes), jnp.float32),
                 pltpu.VMEM((n_block, 8, genes), jnp.float32),
                 pltpu.VMEM((n_gene, 8, genes), jnp.float32),
                 dma((steps, 2)), dma((steps, 2)), dma((steps, 2)), dma((steps, 2)),
+                dma((2, 2)), dma((2, 2)), dma((2, 2)), dma((2, 2)),
                 dma((n_block,)), dma((n_block,)), dma((n_gene,)), dma((n_gene,)),
             ],
             compiler_params=pltpu.CompilerParams(
@@ -266,7 +306,16 @@
                 flops=flops, bytes_accessed=local_rows * samples * 2, transcendentals=0
             ),
         )(genotypes[0], phenotypes, perm_rows, starts.reshape(1, genes))
-        return maxima, moments, pooled.reshape(2)
+        return pl.pallas_call(
+            unpack,
+            out_shape=(
+                jax.ShapeDtypeStruct((width, genes), jnp.float32),
+                jax.ShapeDtypeStruct((2, genes), jnp.float32),
+                jax.ShapeDtypeStruct((2,), jnp.float32),
+            ),
+            in_specs=[vmem],
+            out_specs=(vmem, vmem, pl.BlockSpec(memory_space=pltpu.SMEM)),
+        )(packed)
 
     return jax.shard_map(
         shards,

time: 73.1 us -> 70.7 us (0.967)
  local copies, waits for them, and re-layouts: 2.54 us -> 0 us
  Pallas kernels: 68.3 us -> 69.8 us
  other arithmetic: 1.28 us -> 0 us
    unnamed x2 -> x0, local copies, waits for them, and re-layouts: 2.54 us -> none
    pallas_call x0 -> x1, Pallas kernels: none -> 1.35 us  [shards(): pl.pallas_call(unpack, out_shape=(jax.ShapeDtypeStruct((width, genes), jn...]
    pallas_call x1 -> x0, other arithmetic: 1.28 us -> none  [shards(): pl.pallas_call(functools.partial(kernel, (n_gene, n_var, n_perm)), out_sh...]
where the time goes in v2:
time: 70.7 us; the launch traced here: 70.5 us
  Pallas kernels  69.8 us (99%)
    pallas_call x1, Pallas kernels, shards(): pl.pallas_call(functools.partial(kernel, (n_gene, n_var, n_perm)), out_sh...  68.5 us

profile of v2, /device:TPU:0, one launch (start us, length us, event | category | flops | bytes accessed | tf_op | source)
XLA Modules:
  0.0 70.5 jit_solution(11353110833288217997)
XLA Ops:
  0.6 68.5 %shard_map.67.packed = f32[40,128]{1,0:T(8,128)} custom-call(bf16[768,768]{1,0:T(8,128)(2,1)} %bitcast.2, f32[128,768]{1,0:T(8,128)} %pheno.1, s32[32,768]{1,0:T(8,128)} %perms.1, s32[1,128]{1,0:T(1,128)} %bitcast.3), custom_call_target="tpu_custom_call" | custom-call | flops 43486543872 | bytes 1179648 | tf_op jit(solution)/shard_map/pallas_call | solution.py:285
  69.1 1.3 %shard_map.68 = (f32[32,128]{1,0:T(8,128)}, f32[2,128]{1,0:T(2,128)}, f32[2]{0:T(128)}) custom-call(f32[40,128]{1,0:T(8,128)} %shard_map.67.packed), custom_call_target="tpu_custom_call" | custom-call | tf_op jit(solution)/shard_map/pallas_call | solution.py:309
